TPU v7x, 32 devices: a whole 2x2x4 slice. The times are simulated.
32 devices in a mesh: groups: 2 (over y), src: 4 (over z), tgt: 2 (over x), ill: 2 (over core).
Axes of the slice: x: 2, y: 2, z: 4, core: 2. Of those that a mesh axis runs over, the one named last changes fastest.
Arguments:
- coeffs: bfloat16 [2, 64, 8, 8, 512], P(None, ('groups', 'ill'), 'src', 'tgt'), parts along dimension 1, may hold values from -6 to 6
- reflection: float32 [2, 16, 8, 512], P(None, ('groups', 'src'), 'tgt'), parts along dimension 1, may hold values from -4.2 to 4.2
- interp: float32 [2, 3, 2, 2, 3, 8, 8], replicated, may hold values from -1 to 1
- orders: int32 [512], replicated, may hold values from 0 to 511, each once
Outputs:
- far_field: bfloat16 [2, 64, 8, 8, 512], P(None, ('groups', 'ill'), 'src', 'tgt'), parts along dimension 1
There are 2 independent parts, one for each index of `groups`. A program takes and returns all parts, laid end to end along the dimension named above; an argument that names none is the same for every part. Nothing has to cross between parts.
Inputs may be any that keep to these rules, and one draw needn't show every extreme that they name: `orders`: each number below 512 appears exactly once.
All inputs are finite; a program needn't handle non-finite values.
Results may differ from a plain program's by a relative error of at most 0.028.
Values may be sent and summed in bfloat16 or wider, within the bound.
No kernel may reach another device: no remote copies, remote signals or barrier semaphores. Data moves between devices by JAX's collectives and lax.ppermute only.
A program may use at most 64 MiB of HBM per device.

v0:
```python
import math

import jax
import jax.numpy as jnp
from jax import lax
from jax.sharding import PartitionSpec as P

PHASE_RATE = 0.3
ALONG_SECOND = 1.7
DIRECTIONS = ((0.6, 0.48, 0.64), (-0.36, 0.8, 0.48))


def partner_2(value, axis, bit):
    mask = 2**bit
    pairs = [(source, source ^ mask) for source in range(lax.axis_size(axis))]
    return lax.ppermute(value, axis, pairs)


def node_value(digits, order_count):
    return jnp.cos(math.pi * (2.0 * digits.astype(jnp.float32) + 1.0) / (2.0 * order_count))


def node_products(orders, operator_index, order_count):
    square = order_count * order_count
    digit_first = orders // square
    digit_second = orders // order_count % order_count
    digit_third = orders % order_count
    direction = DIRECTIONS[operator_index]
    summed = direction[0] * node_value(digit_first, order_count)
    summed = summed + direction[1] * node_value(digit_second, order_count)
    return summed + direction[2] * node_value(digit_third, order_count)


def phase_table(products, level_index, u_positions, v_positions):
    position = u_positions[:, None] + 0.5 + ALONG_SECOND * (v_positions[None, :] + 0.5)
    angle_table = PHASE_RATE * (level_index + 1) * position[:, :, None] * products[None, None, :]
    return (jnp.cos(angle_table).astype(jnp.bfloat16), jnp.sin(angle_table).astype(jnp.bfloat16))


def modulate(current, cos_part, sin_part):
    real_part = current[0].astype(jnp.float32)
    imag_part = current[1].astype(jnp.float32)
    cos_value = cos_part.astype(jnp.float32)
    sin_value = sin_part.astype(jnp.float32)
    return jnp.stack(
        [
            cos_value * real_part - sin_value * imag_part,
            cos_value * imag_part + sin_value * real_part,
        ]
    ).astype(jnp.bfloat16)


def reflect(current, reflection):
    real_part = current[0].astype(jnp.float32)
    imag_part = current[1].astype(jnp.float32)
    return jnp.stack(
        [
            reflection[0] * real_part - reflection[1] * imag_part,
            reflection[0] * imag_part + reflection[1] * real_part,
        ]
    ).astype(jnp.bfloat16)


def dense_transposed(factors):
    order_count = factors.shape[-1]
    coef_count = order_count**3
    columns = jnp.arange(coef_count, dtype=jnp.int32)
    digit_list = (
        columns // (order_count * order_count),
        columns // order_count % order_count,
        columns % order_count,
    )
    point_index = jnp.arange(order_count, dtype=jnp.int32)
    spread = []
    for dim_index in range(3):
        selector = (point_index[:, None] == digit_list[dim_index][None, :]).astype(factors.dtype)
        spread.append(jnp.dot(factors[dim_index].T, selector, precision=lax.Precision.HIGHEST))
    full_table = spread[0][:, None, None, :] * spread[1][None, :, None, :]
    full_table = full_table * spread[2][None, None, :, :]
    return full_table.reshape(coef_count, coef_count).astype(jnp.bfloat16)


def pair_level(
    current, products, factors, level_index, box_axis, pair_bit, u_positions, v_positions
):
    cos_part, sin_part = phase_table(products, level_index, u_positions, v_positions)
    modulated = modulate(current, cos_part, sin_part)
    full_shape = modulated.shape
    coef_count = full_shape[-1]
    half_span = 2**pair_bit
    split_shape = (
        full_shape[:box_axis]
        + (full_shape[box_axis] // (2 * half_span), 2, half_span)
        + full_shape[box_axis + 1 :]
    )
    halves = modulated.reshape(split_shape)
    lower_half = jnp.take(halves, 0, axis=box_axis + 1)
    upper_half = jnp.take(halves, 1, axis=box_axis + 1)
    outputs = []
    for side_index in range(2):
        lower_matrix = dense_transposed(factors[side_index, 0])
        upper_matrix = dense_transposed(factors[side_index, 1])
        summed = jnp.dot(
            lower_half.reshape(-1, coef_count), lower_matrix, preferred_element_type=jnp.float32
        )
        summed = summed + jnp.dot(
            upper_half.reshape(-1, coef_count), upper_matrix, preferred_element_type=jnp.float32
        )
        outputs.append(summed.reshape(lower_half.shape))
    combined = jnp.stack(outputs, axis=box_axis + 1).reshape(full_shape)
    return combined.astype(jnp.bfloat16)


def swap_level(
    current, products, factors, level_index, pair_bit, on_source, u_positions, v_positions
):
    cos_part, sin_part = phase_table(products, level_index, u_positions, v_positions)
    modulated = modulate(current, cos_part, sin_part)
    coef_count = modulated.shape[-1]
    if on_source:
        own_bit = lax.axis_index("src") >> pair_bit & 1
    else:
        own_bit = lax.axis_index("tgt") >> pair_bit & 1
    chosen = lax.dynamic_index_in_dim(factors, own_bit, 0, keepdims=False)
    own_matrix = dense_transposed(lax.dynamic_index_in_dim(chosen, own_bit, 0, keepdims=False))
    other_matrix = dense_transposed(
        lax.dynamic_index_in_dim(chosen, 1 - own_bit, 0, keepdims=False)
    )
    summed = jnp.dot(
        modulated.reshape(-1, coef_count), own_matrix, preferred_element_type=jnp.float32
    )
    if on_source:
        partner = partner_2(modulated, "src", pair_bit)
    else:
        partner = partner_2(modulated, "tgt", pair_bit)
    summed = summed + jnp.dot(
        partner.reshape(-1, coef_count), other_matrix, preferred_element_type=jnp.float32
    )
    return summed.reshape(modulated.shape).astype(jnp.bfloat16)


def on_device(coeffs, reflection, interp, orders):
    level_count = interp.shape[1]
    order_count = interp.shape[-1]
    boxes_first = coeffs.shape[2]
    boxes_second = coeffs.shape[3]
    source_count = lax.axis_size("src")
    target_count = lax.axis_size("tgt")
    u_positions = (
        lax.axis_index("src") * boxes_first + jnp.arange(boxes_first, dtype=jnp.int32)
    ).astype(jnp.float32)
    v_positions = (
        lax.axis_index("tgt") * boxes_second + jnp.arange(boxes_second, dtype=jnp.int32)
    ).astype(jnp.float32)
    top_first = (boxes_first * source_count).bit_length() - 2
    top_second = (boxes_second * target_count).bit_length() - 2
    local_first = boxes_first.bit_length() - 1
    local_second = boxes_second.bit_length() - 1
    products = node_products(orders, 0, order_count)
    current = coeffs
    for level_index in range(level_count):
        pair_bit = top_first - level_index
        if pair_bit >= local_first:
            current = swap_level(
                current,
                products,
                interp[0, level_index],
                level_index,
                pair_bit - local_first,
                True,
                u_positions,
                v_positions,
            )
        else:
            current = pair_level(
                current,
                products,
                interp[0, level_index],
                level_index,
                2,
                pair_bit,
                u_positions,
                v_positions,
            )
    current = reflect(current, reflection)
    products = node_products(orders, 1, order_count)
    for level_index in range(level_count):
        pair_bit = top_second - level_index
        if pair_bit >= local_second:
            current = swap_level(
                current,
                products,
                interp[1, level_index],
                level_index,
                pair_bit - local_second,
                False,
                u_positions,
                v_positions,
            )
        else:
            current = pair_level(
                current,
                products,
                interp[1, level_index],
                level_index,
                3,
                pair_bit,
                u_positions,
                v_positions,
            )
    return current


def solution(mesh):
    in_specs = (
        P(None, ("groups", "ill"), "src", "tgt", None),
        P(None, ("groups", "src"), "tgt", None),
        P(),
        P(),
    )
    out_specs = P(None, ("groups", "ill"), "src", "tgt", None)
    return jax.shard_map(
        on_device, mesh=mesh, in_specs=in_specs, out_specs=out_specs, check_vma=False
    )
```

profile of v0, /device:TPU:0, one launch (start us, length us, event | category | flops | bytes accessed | tf_op | source)
XLA Modules:
  0.0 70.3 jit_solution(9338893961869967608)
XLA Ops:
  0.8 1.4 %fusion.71 = (f32[2,4,512]{2,1,0:T(4,128)}, f32[2,4,512]{2,1,0:T(4,128)}, f32[2,4,512]{2,1,0:T(4,128)}, f32[2,4,512]{2,1,0:T(4,128)}, f32[2,4,512]{2,1,0:T(4,128...) fusion(f32[512]{0:T(512)S(1)} %get-tuple-element.138, ...), kind=kLoop, calls=%fused_computation.219 | loop fusion | flops 122880 | bytes 200800 | tf_op jit(solution)/shard_map/convert_element_type | solution.py:43
  2.2 1.1 %fusion.10 = (bf16[1,16,2,4,512]{4,3,2,1,0:T(4,128)(2,1)S(1)}, bf16[1,16,2,4,512]{4,3,2,1,0:T(4,128)(2,1)S(1)}) fusion(f32[2,4,512]{2,1,0:T(4,128)S(1)} %get-tuple-element.136, f32[2,4,512]{2,1,0:T(4,128)S(1)} %get-tuple-element.137, bf16[2,16,2,4,512]{4,3,2,1,0:T(4,128)(2,1)} %param.16), kind=kLoop, calls=%fused_computation.89 | loop fusion | flops 655360 | bytes 557056 | tf_op jit(solution)/shard_map/convert.40
  3.4 0.9 %pad_maximum_fusion = bf16[2,16,2,4,512]{4,3,2,1,0:T(4,128)(2,1)} fusion(bf16[1,16,2,4,512]{4,3,2,1,0:T(4,128)(2,1)S(1)} %get-tuple-element.95, bf16[1,16,2,4,512]{4,3,2,1,0:T(4,128)(2,1)S(1)} %get-tuple-element.94), kind=kLoop, calls=%fused_computation.104 | loop fusion | flops 131072 | bytes 524288 | tf_op jit(solution)/shard_map/stack | solution.py:45
  4.3 4.1 %collective-permute-start = (bf16[2,16,2,4,512]{4,3,2,1,0:T(4,128)(2,1)}, bf16[2,16,2,4,512]{4,3,2,1,0:T(4,128)(2,1)}, u32[]{:S(2)}, u32[]{:S(2)}) collective-permute-start(bf16[2,16,2,4,512]{4,3,2,1,0:T(4,128)(2,1)} %pad_maximum_fusion), channel_id=1, source_target_pairs={{0,8},{4,12},{8,0},{12,4},{1,9},{5,13},{9,1},{13,5},{2,10},{6,14},... | collective-permute-start | bytes 786440 | tf_op jit(solution)/shard_map/ppermute | solution.py:16
  19.9 0.9 %multiply_convert_fusion.15 = bf16[8,8,8,512]{3,2,1,0:T(8,128)(2,1)} fusion(f32[8,512]{1,0:T(8,128)S(1)} %fusion.51, f32[8,8,512]{2,1,0:T(8,128)S(1)} %broadcast_multiply_fusion.15), kind=kLoop, calls=%fused_computation.69 | loop fusion | flops 524288 | bytes 671744 | tf_op jit(solution)/shard_map/convert_element_type | solution.py:80
  20.9 0.9 %multiply_convert_fusion.13 = bf16[8,8,8,512]{3,2,1,0:T(8,128)(2,1)} fusion(f32[8,512]{1,0:T(8,128)S(1)} %convolution_bitcast_fusion.33, f32[8,8,512]{2,1,0:T(8,128)S(1)} %broadcast_multiply_fusion.13), kind=kLoop, calls=%fused_computation.67 | loop fusion | flops 524288 | bytes 671744 | tf_op jit(solution)/shard_map/convert_element_type | solution.py:80
  21.8 0.9 %multiply_convert_fusion.12 = bf16[8,8,8,512]{3,2,1,0:T(8,128)(2,1)} fusion(f32[8,512]{1,0:T(8,128)S(1)} %convolution_bitcast_fusion.30, f32[8,8,512]{2,1,0:T(8,128)S(1)} %broadcast_multiply_fusion.12), kind=kLoop, calls=%fused_computation.66 | loop fusion | flops 524288 | bytes 671744 | tf_op jit(solution)/shard_map/convert_element_type | solution.py:80
  25.5 0.9 %multiply_convert_fusion.5 = bf16[8,8,8,512]{3,2,1,0:T(8,128)(2,1)} fusion(f32[8,512]{1,0:T(8,128)S(1)} %convolution_bitcast_fusion.15, f32[8,8,512]{2,1,0:T(8,128)S(1)} %broadcast_multiply_fusion.5), kind=kLoop, calls=%fused_computation.59 | loop fusion | flops 524288 | bytes 671744 | tf_op jit(solution)/shard_map/convert_element_type | solution.py:80
  27.2 0.9 %multiply_convert_fusion.7 = bf16[8,8,8,512]{3,2,1,0:T(8,128)(2,1)} fusion(f32[8,512]{1,0:T(8,128)S(1)} %convolution_bitcast_fusion.21, f32[8,8,512]{2,1,0:T(8,128)S(1)} %broadcast_multiply_fusion.7), kind=kLoop, calls=%fused_computation.61 | loop fusion | flops 524288 | bytes 671744 | tf_op jit(solution)/shard_map/convert_element_type | solution.py:80
  28.2 0.9 %multiply_convert_fusion.6 = bf16[8,8,8,512]{3,2,1,0:T(8,128)(2,1)} fusion(f32[8,512]{1,0:T(8,128)S(1)} %convolution_bitcast_fusion.18, f32[8,8,512]{2,1,0:T(8,128)S(1)} %broadcast_multiply_fusion.6), kind=kLoop, calls=%fused_computation.60 | loop fusion | flops 524288 | bytes 671744 | tf_op jit(solution)/shard_map/convert_element_type | solution.py:80
  31.5 1.0 %convert_element_type.663 = bf16[256,512]{1,0:T(8,128)(2,1)S(1)} reshape(bf16[2,16,2,4,512]{4,3,2,1,0:T(4,128)(2,1)} %pad_maximum_fusion) | data formatting | bytes 524288 | tf_op jit(solution)/shard_map/convert_element_type | solution.py:50
  32.5 1.3 %fusion.195 = f32[256,512]{1,0:T(8,128)S(1)} fusion(bf16[256,512]{1,0:T(8,128)(2,1)S(1)} %convert_element_type.663, bf16[512,512]{1,0:T(8,128)(2,1)} %bitcast.375), kind=kOutput, calls=%fused_computation.408 | convolution fusion | flops 134217728 | bytes 1310720 | tf_op jit(solution)/shard_map/dot_general | solution.py:129
  33.9 1.0 %reshape.945 = bf16[256,512]{1,0:T(8,128)(2,1)S(1)} reshape(bf16[2,16,2,4,512]{4,3,2,1,0:T(4,128)(2,1)} %collective-permute-done) | data formatting | bytes 524288 | tf_op jit(solution)/shard_map/reshape | solution.py:137
  36.3 0.9 %pad_maximum_fusion.1 = bf16[2,16,2,4,512]{4,3,2,1,0:T(4,128)(2,1)} fusion(bf16[1,16,2,4,512]{4,3,2,1,0:T(4,128)(2,1)S(1)} %get-tuple-element.85, bf16[1,16,2,4,512]{4,3,2,1,0:T(4,128)(2,1)S(1)} %get-tuple-element.84), kind=kLoop, calls=%fused_computation.105 | loop fusion | flops 131072 | bytes 524288 | tf_op jit(solution)/shard_map/stack | solution.py:45
  37.1 1.6 %collective-permute-start.1 = (bf16[2,16,2,4,512]{4,3,2,1,0:T(4,128)(2,1)}, bf16[2,16,2,4,512]{4,3,2,1,0:T(4,128)(2,1)}, u32[]{:S(2)}, u32[]{:S(2)}) collective-permute-start(bf16[2,16,2,4,512]{4,3,2,1,0:T(4,128)(2,1)} %pad_maximum_fusion.1), channel_id=1, source_target_pairs={{0,4},{4,0},{8,12},{12,8},{1,5},{5,1},{9,13},{13,9},{2,6},{6,2},{1... | collective-permute-start | bytes 786440 | tf_op jit(solution)/shard_map/ppermute | solution.py:16
  38.7 1.5 %convolution_bitcast_fusion = f32[8,512]{1,0:T(8,128)} fusion(s32[512]{0:T(512)S(1)} %copy-done.14, f32[2,2,3,8,8]{4,3,2,1,0:T(8,128)} %copy-done.25), kind=kOutput, calls=%fused_computation.18 | convolution fusion | flops 397312 | bytes 22528 | tf_op jit(solution)/shard_map/dot_general | solution.py:77
  40.2 1.0 %convert_element_type.675 = bf16[256,512]{1,0:T(8,128)(2,1)S(1)} reshape(bf16[2,16,2,4,512]{4,3,2,1,0:T(4,128)(2,1)} %pad_maximum_fusion.1) | data formatting | bytes 524288 | tf_op jit(solution)/shard_map/convert_element_type | solution.py:50
  41.5 3.7 %collective-permute-done.1 = bf16[2,16,2,4,512]{4,3,2,1,0:T(4,128)(2,1)} collective-permute-done((bf16[2,16,2,4,512]{4,3,2,1,0:T(4,128)(2,1)}, bf16[2,16,2,4,512]{4,3,2,1,0:T(4,128)(2,1)}, u32[]{:S(2)}, u32[]{:S(2)}) %collective-permute-start.1) | collective-permute-done | bytes 262176 | tf_op jit(solution)/shard_map/ppermute | solution.py:16
  45.2 1.0 %reshape.946 = bf16[256,512]{1,0:T(8,128)(2,1)S(1)} reshape(bf16[2,16,2,4,512]{4,3,2,1,0:T(4,128)(2,1)} %collective-permute-done.1) | data formatting | bytes 524288 | tf_op jit(solution)/shard_map/reshape | solution.py:137
  51.7 0.9 %pad_maximum_fusion.2 = bf16[2,16,2,4,512]{4,3,2,1,0:T(4,128)(2,1)} fusion(bf16[1,16,2,4,512]{4,3,2,1,0:T(4,128)(2,1)S(1)} %fusion.16, bf16[1,16,2,4,512]{4,3,2,1,0:T(4,128)(2,1)S(1)} %get-tuple-element.77), kind=kLoop, calls=%fused_computation.110 | loop fusion | flops 131072 | bytes 524288 | tf_op jit(solution)/shard_map/stack | solution.py:45
  52.6 1.5 %collective-permute-start.2 = (bf16[2,16,2,4,512]{4,3,2,1,0:T(4,128)(2,1)}, bf16[2,16,2,4,512]{4,3,2,1,0:T(4,128)(2,1)}, u32[]{:S(2)}, u32[]{:S(2)}) collective-permute-start(bf16[2,16,2,4,512]{4,3,2,1,0:T(4,128)(2,1)} %pad_maximum_fusion.2), channel_id=1, source_target_pairs={{0,2},{2,0},{1,3},{3,1},{4,6},{6,4},{5,7},{7,5},{8,10},{10,8},{9,1... | collective-permute-start | bytes 786440 | tf_op jit(solution)/shard_map/ppermute | solution.py:16
  54.2 1.0 %convert_element_type.703 = bf16[256,512]{1,0:T(8,128)(2,1)S(1)} reshape(bf16[2,16,2,4,512]{4,3,2,1,0:T(4,128)(2,1)} %pad_maximum_fusion.2) | data formatting | bytes 524288 | tf_op jit(solution)/shard_map/convert_element_type | solution.py:50
  55.5 4.3 %collective-permute-done.2 = bf16[2,16,2,4,512]{4,3,2,1,0:T(4,128)(2,1)} collective-permute-done((bf16[2,16,2,4,512]{4,3,2,1,0:T(4,128)(2,1)}, bf16[2,16,2,4,512]{4,3,2,1,0:T(4,128)(2,1)}, u32[]{:S(2)}, u32[]{:S(2)}) %collective-permute-start.2) | collective-permute-done | bytes 262176 | tf_op jit(solution)/shard_map/ppermute | solution.py:16
  59.8 1.0 %reshape.949 = bf16[256,512]{1,0:T(8,128)(2,1)S(1)} reshape(bf16[2,16,2,4,512]{4,3,2,1,0:T(4,128)(2,1)} %collective-permute-done.2) | data formatting | bytes 524288 | tf_op jit(solution)/shard_map/reshape | solution.py:137
  (209 shorter events, 34.9 us)
Async XLA Ops:
  3.4 5.0 %copy-start.11 = (f32[2,3,2,2,3,8,8]{6,5,4,3,2,1,0:T(8,128)S(1)}, f32[2,3,2,2,3,8,8]{6,5,4,3,2,1,0:T(8,128)}, u32[]{:S(2)}) copy-start(f32[2,3,2,2,3,8,8]{6,5,4,3,2,1,0:T(8,128)} %param.18) | copy-start | bytes 55300
  4.3 29.6 %collective-permute-start = (bf16[2,16,2,4,512]{4,3,2,1,0:T(4,128)(2,1)}, bf16[2,16,2,4,512]{4,3,2,1,0:T(4,128)(2,1)}, u32[]{:S(2)}, u32[]{:S(2)}) collective-permute-start(bf16[2,16,2,4,512]{4,3,2,1,0:T(4,128)(2,1)} %pad_maximum_fusion), channel_id=1, source_target_pairs={{0,8},{4,12},{8,0},{12,4},{1,9},{5,13},{9,1},{13,5},{2,10},{6,14},... | collective-permute-start | bytes 786440 | tf_op jit(solution)/shard_map/ppermute | solution.py:16
  8.3 9.9 %copy-start.13 = (s32[512]{0:T(512)}, s32[512]{0:T(512)S(1)}, u32[]{:S(2)}) copy-start(s32[512]{0:T(512)S(1)} %get-tuple-element.143) | copy-start | bytes 6148
  8.4 10.3 %copy-start.25 = (f32[2,2,3,8,8]{4,3,2,1,0:T(8,128)}, f32[2,2,3,8,8]{4,3,2,1,0:T(8,128)S(1)}, u32[]{:S(2)}) copy-start(f32[2,2,3,8,8]{4,3,2,1,0:T(8,128)S(1)} %get-tuple-element.86) | copy-start | bytes 9220
  30.1 0.8 %copy-start.26 = (f32[2,2,4,512]{3,2,1,0:T(4,128)S(1)}, f32[2,2,4,512]{3,2,1,0:T(4,128)}, u32[]{:S(2)}) copy-start(f32[2,2,4,512]{3,2,1,0:T(4,128)} %param.17) | copy-start | bytes 98308
  35.4 0.7 %copy-start.22 = (f32[2,4,512]{2,1,0:T(4,128)S(1)}, f32[2,4,512]{2,1,0:T(4,128)}, u32[]{:S(2)}) copy-start(f32[2,4,512]{2,1,0:T(4,128)} %get-tuple-element.129) | copy-start | bytes 49156
  36.1 2.6 %copy-start.14 = (s32[512]{0:T(512)S(1)}, s32[512]{0:T(512)}, u32[]{:S(2)}) copy-start(s32[512]{0:T(512)} %copy-done.13) | copy-start | bytes 6148
  36.2 5.0 %copy-start.10 = (bf16[8,8,8,512]{3,2,1,0:T(8,128)(2,1)S(1)}, bf16[8,8,8,512]{3,2,1,0:T(8,128)(2,1)}, u32[]{:S(2)}) copy-start(bf16[8,8,8,512]{3,2,1,0:T(8,128)(2,1)} %multiply_convert_fusion.15) | copy-start | bytes 1572868
  37.1 8.1 %collective-permute-start.1 = (bf16[2,16,2,4,512]{4,3,2,1,0:T(4,128)(2,1)}, bf16[2,16,2,4,512]{4,3,2,1,0:T(4,128)(2,1)}, u32[]{:S(2)}, u32[]{:S(2)}) collective-permute-start(bf16[2,16,2,4,512]{4,3,2,1,0:T(4,128)(2,1)} %pad_maximum_fusion.1), channel_id=1, source_target_pairs={{0,4},{4,0},{8,12},{12,8},{1,5},{5,1},{9,13},{13,9},{2,6},{6,2},{1... | collective-permute-start | bytes 786440 | tf_op jit(solution)/shard_map/ppermute | solution.py:16
  46.7 0.7 %copy-start.20 = (f32[2,4,512]{2,1,0:T(4,128)S(1)}, f32[2,4,512]{2,1,0:T(4,128)}, u32[]{:S(2)}) copy-start(f32[2,4,512]{2,1,0:T(4,128)} %get-tuple-element.117) | copy-start | bytes 49156
  47.6 1.0 %copy-start.2 = (bf16[8,8,8,512]{3,2,1,0:T(8,128)(2,1)S(1)}, bf16[8,8,8,512]{3,2,1,0:T(8,128)(2,1)}, u32[]{:S(2)}) copy-start(bf16[8,8,8,512]{3,2,1,0:T(8,128)(2,1)} %multiply_convert_fusion.13) | copy-start | bytes 1572868
  47.9 1.1 %copy-start.8 = (bf16[8,8,8,512]{3,2,1,0:T(8,128)(2,1)S(1)}, bf16[8,8,8,512]{3,2,1,0:T(8,128)(2,1)}, u32[]{:S(2)}) copy-start(bf16[8,8,8,512]{3,2,1,0:T(8,128)(2,1)} %multiply_convert_fusion.12) | copy-start | bytes 1572868
  48.9 1.0 %copy-start.3 = (bf16[8,8,8,512]{3,2,1,0:T(8,128)(2,1)S(1)}, bf16[8,8,8,512]{3,2,1,0:T(8,128)(2,1)}, u32[]{:S(2)}) copy-start(bf16[8,8,8,512]{3,2,1,0:T(8,128)(2,1)} %multiply_convert_fusion.11) | copy-start | bytes 1572868
  49.2 1.1 %copy-start.9 = (bf16[8,8,8,512]{3,2,1,0:T(8,128)(2,1)S(1)}, bf16[8,8,8,512]{3,2,1,0:T(8,128)(2,1)}, u32[]{:S(2)}) copy-start(bf16[8,8,8,512]{3,2,1,0:T(8,128)(2,1)} %multiply_convert_fusion.10) | copy-start | bytes 1572868
  50.5 0.7 %copy-start.23 = (f32[2,4,512]{2,1,0:T(4,128)S(1)}, f32[2,4,512]{2,1,0:T(4,128)}, u32[]{:S(2)}) copy-start(f32[2,4,512]{2,1,0:T(4,128)} %get-tuple-element.110) | copy-start | bytes 49156
  50.6 0.7 %copy-start.24 = (f32[2,4,512]{2,1,0:T(4,128)S(1)}, f32[2,4,512]{2,1,0:T(4,128)}, u32[]{:S(2)}) copy-start(f32[2,4,512]{2,1,0:T(4,128)} %get-tuple-element.111) | copy-start | bytes 49156
  51.7 2.4 %copy-start.27 = (f32[8,512]{1,0:T(8,128)S(1)}, f32[8,512]{1,0:T(8,128)}, u32[]{:S(2)}) copy-start(f32[8,512]{1,0:T(8,128)} %convolution_bitcast_fusion) | copy-start | bytes 49156
  52.6 2.6 %copy-start.7 = (bf16[8,8,8,512]{3,2,1,0:T(8,128)(2,1)S(1)}, bf16[8,8,8,512]{3,2,1,0:T(8,128)(2,1)}, u32[]{:S(2)}) copy-start(bf16[8,8,8,512]{3,2,1,0:T(8,128)(2,1)} %multiply_convert_fusion.9) | copy-start | bytes 1572868
  52.6 7.2 %collective-permute-start.2 = (bf16[2,16,2,4,512]{4,3,2,1,0:T(4,128)(2,1)}, bf16[2,16,2,4,512]{4,3,2,1,0:T(4,128)(2,1)}, u32[]{:S(2)}, u32[]{:S(2)}) collective-permute-start(bf16[2,16,2,4,512]{4,3,2,1,0:T(4,128)(2,1)} %pad_maximum_fusion.2), channel_id=1, source_target_pairs={{0,2},{2,0},{1,3},{3,1},{4,6},{6,4},{5,7},{7,5},{8,10},{10,8},{9,1... | collective-permute-start | bytes 786440 | tf_op jit(solution)/shard_map/ppermute | solution.py:16
  62.5 1.0 %copy-start = (bf16[8,8,8,512]{3,2,1,0:T(8,128)(2,1)S(1)}, bf16[8,8,8,512]{3,2,1,0:T(8,128)(2,1)}, u32[]{:S(2)}) copy-start(bf16[8,8,8,512]{3,2,1,0:T(8,128)(2,1)} %multiply_convert_fusion.5) | copy-start | bytes 1572868
  62.8 1.1 %copy-start.5 = (bf16[8,8,8,512]{3,2,1,0:T(8,128)(2,1)S(1)}, bf16[8,8,8,512]{3,2,1,0:T(8,128)(2,1)}, u32[]{:S(2)}) copy-start(bf16[8,8,8,512]{3,2,1,0:T(8,128)(2,1)} %multiply_convert_fusion.4) | copy-start | bytes 1572868
  63.9 1.0 %copy-start.1 = (bf16[8,8,8,512]{3,2,1,0:T(8,128)(2,1)S(1)}, bf16[8,8,8,512]{3,2,1,0:T(8,128)(2,1)}, u32[]{:S(2)}) copy-start(bf16[8,8,8,512]{3,2,1,0:T(8,128)(2,1)} %multiply_convert_fusion.7) | copy-start | bytes 1572868
  64.2 1.1 %copy-start.6 = (bf16[8,8,8,512]{3,2,1,0:T(8,128)(2,1)S(1)}, bf16[8,8,8,512]{3,2,1,0:T(8,128)(2,1)}, u32[]{:S(2)}) copy-start(bf16[8,8,8,512]{3,2,1,0:T(8,128)(2,1)} %multiply_convert_fusion.6) | copy-start | bytes 1572868
  66.9 1.0 %copy-start.4 = (bf16[8,8,8,512]{3,2,1,0:T(8,128)(2,1)S(1)}, bf16[8,8,8,512]{3,2,1,0:T(8,128)(2,1)}, u32[]{:S(2)}) copy-start(bf16[8,8,8,512]{3,2,1,0:T(8,128)(2,1)} %multiply_convert_fusion.2) | copy-start | bytes 1572868
  (8 other events, 5.7 us)
where the time goes:
time: 71.4 us; the launch traced here: 70.3 us
  local copies, waits for them, and re-layouts  18.6 us (26%)
  other arithmetic  18.2 us (25%)
  matrix products  17.5 us (25%)
  waiting for transfers between devices  8.02 us (11%)
  starting transfers between devices  7.13 us (10%)
  between operations  0.79 us (1%)
    dot_general x54, matrix products, dense_transposed(): jnp.dot(factors[dim_index].T, selector, precision=lax.Precision.HIGHEST)  11.9 us
    convert_element_type x18, other arithmetic, dense_transposed(): return full_table.reshape(coef_count, coef_count).astype(jnp.bfloat16)  11 us
    unnamed x60, local copies, waits for them, and re-layouts  9.03 us
    ppermute x3, waiting for transfers between devices, partner_2(): return lax.ppermute(value, axis, pairs)  8.02 us
    ppermute x3, starting transfers between devices, partner_2(): return lax.ppermute(value, axis, pairs)  7.13 us
    convert_element_type x3, local copies, waits for them, and re-layouts, modulate(): return jnp.stack([cos_value * real_part - sin_value * imag_part, cos_valu...  3.05 us
    reshape x3, local copies, waits for them, and re-layouts, swap_level(): partner.reshape(-1, coef_count)  3.05 us
    another operation x4, other arithmetic, modulate(): jnp.stack([cos_value * real_part - sin_value * imag_part, cos_value * ima...  2.81 us
  transfers between devices with their start and end apart: 3, of which 2 were waited for; matrix products, arithmetic and copies ran while one was open for 41% of the time, Pallas kernels for 0%

commit v1 on v0

v1 whole, which is shorter than its diff:
```python
import functools
import math

import jax
import jax.numpy as jnp
from jax import lax
from jax.experimental import pallas as pl
from jax.experimental.pallas import tpu as pltpu
from jax.sharding import PartitionSpec as P

PHASE_RATE = 0.3
ALONG_SECOND = 1.7
DIRECTIONS = ((0.6, 0.48, 0.64), (-0.36, 0.8, 0.48))
F32 = jnp.float32
BF16 = jnp.bfloat16


def partner_2(value, axis, bit):
    mask = 2**bit
    pairs = [(source, source ^ mask) for source in range(lax.axis_size(axis))]
    return lax.ppermute(value, axis, pairs)


def node_value(digits, order_count):
    return jnp.cos(math.pi * (2.0 * digits.astype(F32) + 1.0) / (2.0 * order_count))


def node_products(orders, operator_index, order_count):
    square = order_count * order_count
    direction = DIRECTIONS[operator_index]
    summed = direction[0] * node_value(orders // square, order_count)
    summed = summed + direction[1] * node_value(orders // order_count % order_count, order_count)
    return summed + direction[2] * node_value(orders % order_count, order_count)


def plan_levels(level_count, extents, locals_):
    levels = []
    for operator in range(2):
        top = extents[operator].bit_length() - 2
        local_bits = locals_[operator].bit_length() - 1
        for level in range(level_count):
            bit = top - level
            if bit >= local_bits:
                levels.append((operator, level, ("src", "tgt")[operator], bit - local_bits))
            else:
                levels.append((operator, level, None, bit))
    return levels


def build_body(which_ref, spread_ref, w_ref):
    order_count = spread_ref.shape[2]
    first, second, third = spread_ref[0, 0], spread_ref[0, 1], spread_ref[0, 2]
    square = order_count * order_count
    for x in range(order_count):
        lead = first[x : x + 1] * second
        for y in range(0, order_count, 2):
            rows = jnp.concatenate([lead[y : y + 1] * third, lead[y + 1 : y + 2] * third])
            w_ref[0, x * square + y * order_count : x * square + (y + 2) * order_count] = rows.astype(BF16)


def build_matrices(spread, which):
    count = which.shape[0]
    _, dims, order_count, coef_count = spread.shape
    return pl.pallas_call(
        build_body,
        grid_spec=pltpu.PrefetchScalarGridSpec(
            num_scalar_prefetch=1,
            grid=(count,),
            in_specs=[pl.BlockSpec((1, dims, order_count, coef_count), lambda m, w: (w[m], 0, 0, 0))],
            out_specs=pl.BlockSpec((1, coef_count, coef_count), lambda m, w: (m, 0, 0)),
        ),
        out_shape=jax.ShapeDtypeStruct((count, coef_count, coef_count), BF16),
        compiler_params=pltpu.CompilerParams(vmem_limit_bytes=8 * 1024 * 1024),
        cost_estimate=pl.CostEstimate(
            flops=count * 2 * coef_count * coef_count, bytes_accessed=count * 2 * coef_count * coef_count, transcendentals=0
        ),
        name="build_matrices",
    )(which, spread)


def modulate(src, table, index, dst, boxes, ill, place):
    half = boxes * ill
    for box in range(boxes):
        real = src[box * ill : (box + 1) * ill].astype(F32)
        imag = src[half + box * ill : half + (box + 1) * ill].astype(F32)
        cos = table[index, 0, box : box + 1]
        sin = table[index, 1, box : box + 1]
        dst[place(0, box)] = (cos * real - sin * imag).astype(BF16)
        dst[place(1, box)] = (cos * imag + sin * real).astype(BF16)


def straight(boxes, ill):
    half = boxes * ill
    return lambda part, box: pl.ds(part * half + box * ill, ill)


def dot(a, b):
    return jnp.dot(a, b, preferred_element_type=F32)


def own_body(shape, index, raw, x_ref, table_ref, w_ref, out_ref, mod_ref):
    boxes, ill = shape
    if raw:
        modulate(x_ref, table_ref, index, mod_ref, boxes, ill, straight(boxes, ill))
        out_ref[...] = dot(mod_ref[...], w_ref[...])
    else:
        out_ref[...] = dot(x_ref[...], w_ref[...])


def rest_body(shape, partner_index, pairs, send_index, *refs):
    boxes_u, boxes_v, ill = shape
    boxes = boxes_u * boxes_v
    half = boxes * ill
    part_ref, got_ref, table_ref, w_ref = refs[:4]
    pair_refs = refs[4 : 4 + len(pairs)]
    out_ref, state_ref, mod_ref = refs[4 + len(pairs) :]
    if partner_index is None:
        got = got_ref[...]
    else:
        modulate(got_ref, table_ref, partner_index, mod_ref, boxes, ill, straight(boxes, ill))
        got = mod_ref[...]
    state_ref[...] = part_ref[...] + dot(got, w_ref[...])
    for number, (index, operator, bit) in enumerate(pairs):
        w4_ref = pair_refs[number]
        box_bit = bit + (boxes_v.bit_length() - 1 if operator == 0 else 0)
        low_mask = (1 << box_bit) - 1

        def place(part, box):
            side = box >> box_bit & 1
            rank = (box >> (box_bit + 1) << box_bit) | (box & low_mask)
            return pl.ds(side * half + part * (half // 2) + rank * ill, ill)

        modulate(state_ref, table_ref, index, mod_ref, boxes, ill, place)
        for side in range(2):
            result = dot(mod_ref[:half], w4_ref[2 * side]) + dot(mod_ref[half:], w4_ref[2 * side + 1])
            for part in range(2):
                for box in range(boxes):
                    if box >> box_bit & 1 == side:
                        begin = place(part, box).start - side * half
                        state_ref[straight(boxes, ill)(part, box)] = result[begin : begin + ill]
    if send_index is None:
        out_ref[...] = state_ref[...].astype(BF16)
    else:
        modulate(state_ref, table_ref, send_index, out_ref, boxes, ill, straight(boxes, ill))


def call(body, outs, scratch, flops, moved, name, *args):
    return pl.pallas_call(
        body,
        out_shape=outs,
        in_specs=[pl.BlockSpec(memory_space=pltpu.VMEM)] * len(args),
        out_specs=pl.BlockSpec(memory_space=pltpu.VMEM),
        scratch_shapes=scratch,
        compiler_params=pltpu.CompilerParams(vmem_limit_bytes=24 * 1024 * 1024),
        cost_estimate=pl.CostEstimate(flops=flops, bytes_accessed=moved, transcendentals=0),
        name=name,
    )(*args)


def on_device(coeffs, reflection, interp, orders):
    level_count = interp.shape[1]
    order_count = interp.shape[-1]
    _, ill, boxes_u, boxes_v, coef_count = coeffs.shape
    boxes = boxes_u * boxes_v
    rows = 2 * boxes * ill
    extents = (boxes_u * lax.axis_size("src"), boxes_v * lax.axis_size("tgt"))
    levels = plan_levels(level_count, extents, (boxes_u, boxes_v))
    assert levels[0][2] is not None

    partner_raw = partner_2(coeffs, levels[0][2], levels[0][3])

    place = {"src": lax.axis_index("src"), "tgt": lax.axis_index("tgt")}

    def positions(src, tgt):
        u = (src * boxes_u + jnp.arange(boxes_u, dtype=jnp.int32)).astype(F32)
        v = (tgt * boxes_v + jnp.arange(boxes_v, dtype=jnp.int32)).astype(F32)
        return (u[:, None] + 0.5 + ALONG_SECOND * (v[None, :] + 0.5)).reshape(boxes)

    own_position = positions(place["src"], place["tgt"])
    other_position = positions(place["src"] ^ 2 ** levels[0][3], place["tgt"])
    products = [node_products(orders, operator, order_count) for operator in range(2)]
    scales = jnp.stack(
        [PHASE_RATE * (level + 1) * own_position for _, level, _, _ in levels] + [PHASE_RATE * other_position]
    )
    by_level = jnp.stack([products[operator] for operator, _, _, _ in levels] + [products[0]])
    angles = scales[:, :, None] * by_level[:, None, :]
    cos = jnp.cos(angles).astype(BF16).astype(F32)
    sin = jnp.sin(angles).astype(BF16).astype(F32)
    reflect = reflection.reshape(2, boxes, coef_count)
    first = next(i for i, level in enumerate(levels) if level[0] == 1)
    mark = (jnp.arange(len(levels) + 1) == first)[:, None, None]
    table = jnp.stack(
        [
            jnp.where(mark, cos * reflect[0] - sin * reflect[1], cos),
            jnp.where(mark, cos * reflect[1] + sin * reflect[0], sin),
        ],
        axis=1,
    )

    columns = jnp.arange(coef_count, dtype=jnp.int32)
    digits = (columns // (order_count * order_count), columns // order_count % order_count, columns % order_count)
    points = jnp.arange(order_count, dtype=jnp.int32)
    factors = interp.reshape(-1, 3, order_count, order_count)
    spread = jnp.stack(
        [
            lax.dot_general(
                factors[:, d],
                (points[:, None] == digits[d][None, :]).astype(F32),
                (((1,), (0,)), ((), ())),
                precision=lax.Precision.HIGHEST,
            )
            for d in range(3)
        ],
        axis=1,
    )
    which, offset = [], []
    for operator, level, axis, bit in levels:
        base = (operator * level_count + level) * 4
        offset.append(len(which))
        if axis is None:
            which += [base, base + 1, base + 2, base + 3]
        else:
            own = lax.axis_index(axis) >> bit & 1
            which += [base + 3 * own, base + 2 * own + (1 - own)]
    which = jnp.stack([jnp.asarray(w, jnp.int32) for w in which])
    matrices = build_matrices(spread, which)

    def rowwise(value):
        return value.transpose(0, 2, 3, 1, 4).reshape(rows, coef_count)

    product_flops = 2 * rows * coef_count * coef_count
    swaps = [i for i, level in enumerate(levels) if level[2] is not None]
    current, partner = rowwise(coeffs), None
    for number, index in enumerate(swaps):
        _, _, axis, bit = levels[index]
        raw = number == 0
        partner = rowwise(partner_raw) if raw else partner_2(current, axis, bit)
        own = call(
            functools.partial(own_body, (boxes, ill), index, raw),
            jax.ShapeDtypeStruct((rows, coef_count), F32),
            [pltpu.VMEM((rows, coef_count), BF16)],
            product_flops,
            rows * coef_count * 6 + coef_count * coef_count * 2,
            f"own_{index}",
            current,
            table,
            matrices[offset[index]],
        )
        after = swaps[number + 1] if number + 1 < len(swaps) else len(levels)
        pairs = [(i, levels[i][0], levels[i][3]) for i in range(index + 1, after)]
        current = call(
            functools.partial(
                rest_body,
                (boxes_u, boxes_v, ill),
                len(levels) if raw else None,
                pairs,
                after if after < len(levels) else None,
            ),
            jax.ShapeDtypeStruct((rows, coef_count), BF16),
            [pltpu.VMEM((rows, coef_count), F32), pltpu.VMEM((rows, coef_count), BF16)],
            product_flops * (1 + 2 * len(pairs)),
            rows * coef_count * 8 + coef_count * coef_count * 2 * (1 + 4 * len(pairs)),
            f"rest_{index}",
            own,
            partner,
            table,
            matrices[offset[index] + 1],
            *[matrices[offset[i] : offset[i] + 4] for i, _, _ in pairs],
        )
    return current.reshape(2, boxes_u, boxes_v, ill, coef_count).transpose(0, 3, 1, 2, 4)


def solution(mesh):
    in_specs = (
        P(None, ("groups", "ill"), "src", "tgt", None),
        P(None, ("groups", "src"), "tgt", None),
        P(),
        P(),
    )
    out_specs = P(None, ("groups", "ill"), "src", "tgt", None)
    return jax.shard_map(
        on_device, mesh=mesh, in_specs=in_specs, out_specs=out_specs, check_vma=False
    )
```

time: 71.4 us -> 34.1 us (0.48)
  other arithmetic: 18.2 us -> 1.49 us
  local copies, waits for them, and re-layouts: 18.6 us -> 4.06 us
  matrix products: 17.5 us -> 3.79 us
  Pallas kernels: 0 us -> 5.63 us
  waiting for transfers between devices: 8.02 us -> 12.1 us
  starting transfers between devices: 7.13 us -> 6.36 us
    dot_general x72 -> x3, matrix products: 17.5 us -> 3.79 us  [on_device(): lax.dot_general(factors[:, d], (points[:, None] == digits[d][None, :]).as...]
    convert_element_type x22 -> x0, other arithmetic: 12.6 us -> none  [the longest x18 11 us: dense_transposed(): return full_table.reshape(coef_count, coef_count).astype(jnp.bfloat16)]
    unnamed x60 -> x0, local copies, waits for them, and re-layouts: 9.03 us -> none
    pallas_call x0 -> x7, Pallas kernels: none -> 5.63 us  [the longest x6 3.12 us: call(): pl.pallas_call(body, out_shape=outs, in_specs=[pl.BlockSpec(memory_space=...]
    another operation x11 -> x2, other arithmetic: 5.07 us -> 0.12 us  [the longest x1 0.1 us: on_device(): jnp.stack([lax.dot_general(factors[:, d], (points[:, None] == digits[d][N...]
    convert_element_type x10 -> x0, local copies, waits for them, and re-layouts: 4.3 us -> none  [the longest x3 3.05 us: modulate(): return jnp.stack([cos_value * real_part - sin_value * imag_part, cos_valu...]
    ppermute x3, waiting for transfers between devices: 8.02 us -> 12.1 us  [partner_2(): return lax.ppermute(value, axis, pairs)]
    reshape x9 -> x1, local copies, waits for them, and re-layouts: 3.35 us -> 0.91 us  [on_device(): current.reshape(2, boxes_u, boxes_v, ill, coef_count)]
  transfers between devices with their start and end apart: 3 -> 3, of which waited for: 2 -> 3; matrix products, arithmetic and copies ran while one was open for 41% -> 25% of each run, Pallas kernels for 0% -> 10%
where the time goes in v1:
time: 34.1 us; the launch traced here: 33.7 us
  waiting for transfers between devices  12.1 us (35%)
  starting transfers between devices  6.36 us (19%)
  Pallas kernels  5.63 us (17%)
  local copies, waits for them, and re-layouts  4.06 us (12%)
  matrix products  3.79 us (11%)
  other arithmetic  1.49 us (4%)
    ppermute x3, waiting for transfers between devices, partner_2(): return lax.ppermute(value, axis, pairs)  12.1 us
    ppermute x3, starting transfers between devices, partner_2(): return lax.ppermute(value, axis, pairs)  6.36 us
    dot_general x3, matrix products, on_device(): lax.dot_general(factors[:, d], (points[:, None] == digits[d][None, :]).as...  3.79 us
    pallas_call x6, Pallas kernels, call(): pl.pallas_call(body, out_shape=outs, in_specs=[pl.BlockSpec(memory_space=...  3.12 us
    pallas_call x1, Pallas kernels, build_matrices(): pl.pallas_call(build_body, grid_spec=pltpu.PrefetchScalarGridSpec(num_sca...  2.51 us
    transpose x2, local copies, waits for them, and re-layouts, rowwise(): return value.transpose(0, 2, 3, 1, 4).reshape(rows, coef_count)  1.11 us
    reshape x1, local copies, waits for them, and re-layouts, on_device(): current.reshape(2, boxes_u, boxes_v, ill, coef_count)  0.91 us
    add x1, other arithmetic, node_products(): return summed + direction[2] * node_value(orders % order_count, order_count)  0.75 us
  transfers between devices with their start and end apart: 3, of which 3 were waited for; matrix products, arithmetic and copies ran while one was open for 25% of the time, Pallas kernels for 10%

profile of v1, /device:TPU:0, one launch (start us, length us, event | category | flops | bytes accessed | tf_op | source)
XLA Modules:
  0.0 33.7 jit_solution(7421835741039665144)
XLA Ops:
  0.0 4.1 %collective-permute-start = (bf16[2,16,2,4,512]{4,3,2,1,0:T(4,128)(2,1)}, bf16[2,16,2,4,512]{4,3,2,1,0:T(4,128)(2,1)S(1)}, u32[]{:S(2)}, u32[]{:S(2)}) collective-permute-start(bf16[2,16,2,4,512]{4,3,2,1,0:T(4,128)(2,1)} %param.4), channel_id=1, source_target_pairs={{0,8},{4,12},{8,0},{12,4},{1,9},{5,13},{9,1},{13,5},{2,10},{6,14},... | collective-permute-start | bytes 786440 | tf_op jit(solution)/shard_map/ppermute | solution.py:21
  4.5 0.8 %multiply_add_fusion = (f32[512]{0:T(512)S(1)}, f32[512]{0:T(512)S(1)}) fusion(s32[512]{0:T(512)} %param.7), kind=kLoop, calls=%fused_computation.80 | loop fusion | flops 31744 | bytes 6144 | tf_op jit(solution)/shard_map/add | solution.py:33
  5.3 0.7 %fusion.38 = (f32[1,2,4,512]{3,2,1,0:T(4,128)S(1)}, f32[1,2,4,512]{3,2,1,0:T(4,128)S(1)}) fusion(f32[2,2,4,512]{3,2,1,0:T(4,128)} %param.5), kind=kLoop, calls=%fused_computation.95 | loop fusion | bytes 65536 | tf_op jit(solution)/shard_map/slice | solution.py:194
  6.1 1.3 %convolution_bitcast_fusion = f32[24,1,8,512]{3,2,1,0:T(8,128)S(1)} fusion(f32[24,3,8,8]{3,2,1,0:T(8,128)} %bitcast.65, s32[512]{0:T(512)S(1)} %add_select_fusion), kind=kOutput, calls=%fused_computation | convolution fusion | flops 9441280 | bytes 493568 | tf_op jit(solution)/shard_map/dot_general | solution.py:206
  7.3 1.3 %convolution_bitcast_fusion.1 = f32[24,1,8,512]{3,2,1,0:T(8,128)S(1)} fusion(f32[24,3,8,8]{3,2,1,0:T(8,128)} %bitcast.66, s32[512]{0:T(512)S(1)} %add_select_fusion.1), kind=kOutput, calls=%fused_computation.1 | convolution fusion | flops 9441280 | bytes 493568 | tf_op jit(solution)/shard_map/dot_general | solution.py:206
  8.6 1.3 %convolution_bitcast_fusion.2 = f32[24,1,8,512]{3,2,1,0:T(8,128)S(1)} fusion(f32[24,3,8,8]{3,2,1,0:T(8,128)} %bitcast.67, s32[512]{0:T(512)S(1)} %add_select_fusion.3), kind=kOutput, calls=%fused_computation.2 | convolution fusion | flops 9441280 | bytes 493568 | tf_op jit(solution)/shard_map/dot_general | solution.py:206
  9.9 1.0 %copy.12 = bf16[2,2,4,16,512]{4,3,2,1,0:T(8,128)(2,1)S(1)} copy(bf16[2,2,4,16,512]{4,2,1,3,0:T(4,128)(2,1)} %bitcast.68) | data formatting | bytes 524288 | tf_op jit(solution)/shard_map/transpose | solution.py:229
  11.0 0.5 %convert_select_fusion.1 = (f32[7,1,8,512]{3,2,1,0:T(8,128)S(1)}, f32[7,1,8,512]{3,2,1,0:T(8,128)S(1)}) fusion(f32[8,512]{1,0:T(8,128)S(1)} %mul.255, f32[8,512]{1,0:T(8,128)S(1)} %mul.252, f32[7,512]{1,0:T(8,128)S(1)} %stack.65, f32[7,8]{1,0:T(8,128)S(1)} %stack.62, pred[7]{0:T(512)(128)(4,1)S(1)} %iota_compare_fusion.3), kind=kLoop, calls=%fused_computation.16 | loop fusion | flops 372736 | bytes 276711 | tf_op jit(solution)/shard_map/jit(_where)/select_n | solution.py:194
  11.6 0.1 stack.73.which_ref
  11.7 2.5 %build_matrices.1 = bf16[18,512,512]{2,1,0:T(8,128)(2,1)S(1)} custom-call(s32[18]{0:T(128)S(1)} %stack.73.which_ref, f32[24,3,8,512]{3,2,1,0:T(8,128)S(1)} %pad_maximum_fusion.spread_ref), custom_call_target="tpu_custom_call" | custom-call | flops 9437184 | bytes 9437184 | tf_op jit(solution)/shard_map/build_matrices/pallas_call | solution.py:64
  14.3 0.4 %slice_bitcast_fusion = (bf16[512,512]{1,0:T(8,128)(2,1)S(1)}, bf16[512,512]{1,0:T(8,128)(2,1)S(1)}, bf16[512,512]{1,0:T(8,128)(2,1)S(1)}, bf16[512,512]{1,0:T(8...) fusion(bf16[18,512,512]{2,1,0:T(8,128)(2,1)S(1)} %build_matrices.1), kind=kLoop, calls=%fused_computation.4 | loop fusion | bytes 6291456 | tf_op jit(solution)/shard_map/squeeze | solution.py:267
  14.6 0.3 own_0.1.refs_0_
  15.0 1.2 %collective-permute-done = bf16[2,16,2,4,512]{4,3,2,1,0:T(4,128)(2,1)S(1)} collective-permute-done((bf16[2,16,2,4,512]{4,3,2,1,0:T(4,128)(2,1)}, bf16[2,16,2,4,512]{4,3,2,1,0:T(4,128)(2,1)S(1)}, u32[]{:S(2)}, u32[]{:S(2)}) %collective-permute-start) | collective-permute-done | bytes 262176 | tf_op jit(solution)/shard_map/ppermute | solution.py:21
  16.3 0.3 %rest_0.1.x_ref = bf16[256,512]{1,0:T(8,128)(2,1)S(1)} custom-call(f32[256,512]{1,0:T(8,128)S(1)} %own_0.1.refs_0_, bf16[256,512]{1,0:T(8,128)(2,1)S(1)} %bitcast.63, f32[7,2,8,512]{3,2,1,0:T(8,128)S(1)} %pad_maximum_fusion.1.table_ref.refs_2_, bf16[512,512]{1,0:T(8,128)(2,1)S(1)} %get-tuple-element.12.refs_3_), custom_call_target="tpu_custom_call" | custom-call | flops 134217728 | bytes 1572864 | tf_op jit(solution)/shard_map/rest_0/pallas_call | solution.py:148
  16.6 0.9 %collective-permute-start.1 = (bf16[256,512]{1,0:T(8,128)(2,1)S(1)}, bf16[256,512]{1,0:T(8,128)(2,1)S(1)}, u32[]{:S(2)}, u32[]{:S(2)}) collective-permute-start(bf16[256,512]{1,0:T(8,128)(2,1)S(1)} %rest_0.1.x_ref), channel_id=1, source_target_pairs={{0,4},{4,0},{8,12},{12,8},{1,5},{5,1},{9,13},{13,9},{2,6},{6,2},{1... | collective-permute-start | bytes 786440 | tf_op jit(solution)/shard_map/ppermute | solution.py:21
  17.5 0.4 %fusion.37 = (bf16[4,512,512]{2,1,0:T(8,128)(2,1)S(1)}, bf16[4,512,512]{2,1,0:T(8,128)(2,1)S(1)}, bf16[4,512,512]{2,1,0:T(8,128)(2,1)S(1)}) fusion(bf16[18,512,512]{2,1,0:T(8,128)(2,1)S(1)} %build_matrices.1), kind=kLoop, calls=%fused_computation.94 | loop fusion | bytes 12582912 | tf_op jit(solution)/shard_map/slice | solution.py:268
  17.9 0.3 own_1.1.refs_0_
  18.2 5.9 %collective-permute-done.1.refs_1_ = bf16[256,512]{1,0:T(8,128)(2,1)S(1)} collective-permute-done((bf16[256,512]{1,0:T(8,128)(2,1)S(1)}, bf16[256,512]{1,0:T(8,128)(2,1)S(1)}, u32[]{:S(2)}, u32[]{:S(2)}) %collective-permute-start.1) | collective-permute-done | bytes 262176 | tf_op jit(solution)/shard_map/ppermute | solution.py:21
  24.2 0.7 %rest_1.1.x_ref = bf16[256,512]{1,0:T(8,128)(2,1)S(1)} custom-call(f32[256,512]{1,0:T(8,128)S(1)} %own_1.1.refs_0_, bf16[256,512]{1,0:T(8,128)(2,1)S(1)} %collective-permute-done.1.refs_1_, f32[7,2,8,512]{3,2,1,0:T(8,128)S(1)} %pad_maximum_fusion.1.table_ref.refs_2_, bf16[512,512]{1,0:T(8,128)(2,1)S(1)} %get-tuple-element.10.refs_3_, ...), custom_call_target="tpu_custom_call" | custom-call | flops 402653184 | bytes 3670016 | tf_op jit(solution)/shard_map/rest_1/pallas_call | solution.py:148
  24.9 1.4 %collective-permute-start.2 = (bf16[256,512]{1,0:T(8,128)(2,1)S(1)}, bf16[256,512]{1,0:T(8,128)(2,1)S(1)}, u32[]{:S(2)}, u32[]{:S(2)}) collective-permute-start(bf16[256,512]{1,0:T(8,128)(2,1)S(1)} %rest_1.1.x_ref), channel_id=1, source_target_pairs={{0,2},{2,0},{1,3},{3,1},{4,6},{6,4},{5,7},{7,5},{8,10},{10,8},{9,1... | collective-permute-start | bytes 786440 | tf_op jit(solution)/shard_map/ppermute | solution.py:21
  26.3 0.3 own_3.1.refs_0_
  26.6 5.0 %collective-permute-done.2.refs_1_ = bf16[256,512]{1,0:T(8,128)(2,1)S(1)} collective-permute-done((bf16[256,512]{1,0:T(8,128)(2,1)S(1)}, bf16[256,512]{1,0:T(8,128)(2,1)S(1)}, u32[]{:S(2)}, u32[]{:S(2)}) %collective-permute-start.2) | collective-permute-done | bytes 262176 | tf_op jit(solution)/shard_map/ppermute | solution.py:21
  31.6 1.1 %rest_3.1 = bf16[256,512]{1,0:T(8,128)(2,1)S(1)} custom-call(f32[256,512]{1,0:T(8,128)S(1)} %own_3.1.refs_0_, bf16[256,512]{1,0:T(8,128)(2,1)S(1)} %collective-permute-done.2.refs_1_, f32[7,2,8,512]{3,2,1,0:T(8,128)S(1)} %pad_maximum_fusion.1.table_ref.refs_2_, bf16[512,512]{1,0:T(8,128)(2,1)S(1)} %get-tuple-element.8.refs_3_, ...), custom_call_target="tpu_custom_call" | custom-call | flops 671088640 | bytes 5767168 | tf_op jit(solution)/shard_map/rest_3/pallas_call | solution.py:148
  32.7 0.9 %copy.34 = bf16[2,2,4,16,512]{4,2,1,3,0:T(4,128)(2,1)} copy(bf16[2,2,4,16,512]{4,3,2,1,0:T(8,128)(2,1)S(1)} %bitcast.62) | data formatting | bytes 524288 | tf_op jit(solution)/shard_map/reshape | solution.py:270
  (18 shorter events, 0.7 us)
Async XLA Ops:
  0.0 16.2 %collective-permute-start = (bf16[2,16,2,4,512]{4,3,2,1,0:T(4,128)(2,1)}, bf16[2,16,2,4,512]{4,3,2,1,0:T(4,128)(2,1)S(1)}, u32[]{:S(2)}, u32[]{:S(2)}) collective-permute-start(bf16[2,16,2,4,512]{4,3,2,1,0:T(4,128)(2,1)} %param.4), channel_id=1, source_target_pairs={{0,8},{4,12},{8,0},{12,4},{1,9},{5,13},{9,1},{13,5},{2,10},{6,14},... | collective-permute-start | bytes 786440 | tf_op jit(solution)/shard_map/ppermute | solution.py:21
  16.6 7.5 %collective-permute-start.1 = (bf16[256,512]{1,0:T(8,128)(2,1)S(1)}, bf16[256,512]{1,0:T(8,128)(2,1)S(1)}, u32[]{:S(2)}, u32[]{:S(2)}) collective-permute-start(bf16[256,512]{1,0:T(8,128)(2,1)S(1)} %rest_0.1.x_ref), channel_id=1, source_target_pairs={{0,4},{4,0},{8,12},{12,8},{1,5},{5,1},{9,13},{13,9},{2,6},{6,2},{1... | collective-permute-start | bytes 786440 | tf_op jit(solution)/shard_map/ppermute | solution.py:21
  24.9 6.7 %collective-permute-start.2 = (bf16[256,512]{1,0:T(8,128)(2,1)S(1)}, bf16[256,512]{1,0:T(8,128)(2,1)S(1)}, u32[]{:S(2)}, u32[]{:S(2)}) collective-permute-start(bf16[256,512]{1,0:T(8,128)(2,1)S(1)} %rest_1.1.x_ref), channel_id=1, source_target_pairs={{0,2},{2,0},{1,3},{3,1},{4,6},{6,4},{5,7},{7,5},{8,10},{10,8},{9,1... | collective-permute-start | bytes 786440 | tf_op jit(solution)/shard_map/ppermute | solution.py:21
